TPU v7x, 32 devices: a whole 2x2x4 slice. The times are simulated.
32 devices in a mesh: lat: 8 (over z, x), lev: 4 (over y, core).
Axes of the slice: x: 2, y: 2, z: 4, core: 2. Of those that a mesh axis runs over, the one named last changes fastest.
Arguments:
- right_side: float32 [8, 64, 2048], P('lev', 'lat'), may hold values from -6 to 6
- diag_shift: float32 [8, 64, 2048], P('lev', 'lat'), may hold values from 0.5 to 2
- level_scale: float32 [8], P('lev'), may hold values from 0.1 to 1
Outputs:
- solution: float32 [8, 64, 2048], P('lev', 'lat')
- residual: float32 [8, 64, 2048], P('lev', 'lat')
All inputs are finite; a program needn't handle non-finite values.
Results may differ from a plain program's by a relative error of at most 0.0003.
Values sent between devices are 32-bit elements; how exact they have to be, the bound alone decides.
A program may use at most 64 MiB of HBM per device.

v0:
```python
import jax
import jax.numpy as jnp
from jax import lax
from jax.sharding import PartitionSpec as P

WAVES = 640
ITERS = 3


def with_halo(block, sides, width):
    for axis, dim in sides:
        count = lax.axis_size(axis)
        forward = [(i, i + 1) for i in range(count - 1)]
        backward = [(target, source) for source, target in forward]
        low = lax.ppermute(
            lax.slice_in_dim(block, block.shape[dim] - width, None, axis=dim), axis, forward
        )
        high = lax.ppermute(lax.slice_in_dim(block, 0, width, axis=dim), axis, backward)
        block = jnp.concatenate([low, block, high], axis=dim)
    return block


def polar_gain(total_rows, start, count):
    latitude = (start + jnp.arange(count, dtype=jnp.int32)).astype(jnp.float32)
    colatitude = jnp.pi * (4.0 * latitude + 3.0) / (4.0 * total_rows + 2.0)
    return 1.0 / jnp.maximum(jnp.sin(colatitude), 0.5) ** 2


def fourier_table(longitudes, wavenumber, cosine_part):
    position = jnp.arange(longitudes, dtype=jnp.int32)
    product = position[:, None] * wavenumber[None, :] % longitudes
    radians = 2.0 * jnp.pi / longitudes * product.astype(jnp.float32)
    return jnp.where(cosine_part[None, :], jnp.cos(radians), jnp.sin(radians))


def sine_table(latitudes):
    counter = jnp.arange(1, latitudes + 1, dtype=jnp.int32)
    product = counter[:, None] * counter[None, :] % (2 * latitudes + 2)
    return jnp.sin(jnp.pi / (latitudes + 1) * product.astype(jnp.float32))


def spectral_weights(latitudes, longitudes, wavenumber):
    counter = jnp.arange(1, latitudes + 1, dtype=jnp.int32).astype(jnp.float32)
    zonal_part = 4.0 * jnp.sin(jnp.pi / longitudes * wavenumber.astype(jnp.float32)) ** 2
    merid_part = 4.0 * jnp.sin(0.5 * jnp.pi / (latitudes + 1) * counter) ** 2
    scaling = 2.0 / (longitudes * (latitudes + 1))
    return scaling / (1.0 + merid_part[:, None] + zonal_part[None, :])


def stencil(padded, diagonal, level_scale, zonal_gain):
    centre = padded[:, 1:-1, :]
    meridional = padded[:, :-2, :] + padded[:, 2:, :]
    zonal_pair = jnp.roll(centre, 1, axis=2) + jnp.roll(centre, -1, axis=2)
    corners = jnp.roll(meridional, 1, axis=2) + jnp.roll(meridional, -1, axis=2)
    coupling = zonal_gain[None, :, None] * zonal_pair + meridional + 0.125 * corners
    return diagonal * centre - level_scale[:, None, None] * coupling


def operate(field, diagonal, level_scale, zonal_gain):
    padded = with_halo(field, (("lat", 1),), 1)
    midway = field.shape[2] // 2
    position = lax.axis_index("lat")
    final_band = lax.axis_size("lat") - 1
    northern = jnp.roll(field[:, :1, :], midway, axis=2)
    southern = jnp.roll(field[:, -1:, :], midway, axis=2)
    upper_row = jnp.where(position == 0, northern, padded[:, :1, :])
    lower_row = jnp.where(position == final_band, southern, padded[:, -1:, :])
    padded = jnp.concatenate([upper_row, padded[:, 1:-1, :], lower_row], axis=1)
    return stencil(padded, diagonal, level_scale, zonal_gain)


def precondition(current, diagonal, fourier, sines, spectral):
    highest = lax.Precision.HIGHEST
    levels, band_rows, longitudes = current.shape
    columns = fourier.shape[1]
    flattened = current.reshape(levels * band_rows, longitudes)
    coefficients = jnp.dot(
        flattened, fourier, precision=highest, preferred_element_type=jnp.float32
    )
    coefficients = coefficients.reshape(levels, band_rows, columns)

    def meridional(received):
        modes = jnp.einsum("kjc,jl->klc", received, sines, precision=highest) * spectral[None]
        returned = jnp.einsum("klc,jl->kjc", modes, sines, precision=highest)
        return lax.all_to_all(returned, "lat", split_axis=1, concat_axis=2, tiled=True)

    arrived = meridional(
        lax.all_to_all(coefficients, "lat", split_axis=2, concat_axis=1, tiled=True)
    )
    synthesis = lax.dot_general(
        arrived.reshape(levels * band_rows, columns),
        fourier,
        (((1,), (1,)), ((), ())),
        precision=highest,
        preferred_element_type=jnp.float32,
    )
    return 0.5 * current / diagonal + synthesis.reshape(levels, band_rows, longitudes)


def paired_products(residual, adjusted, applied):
    return lax.psum((jnp.sum(residual * adjusted), jnp.sum(applied * adjusted)), ("lat", "lev"))


def body(right_side, diag_shift, level_scale):
    levels, band_rows, longitudes = right_side.shape
    bands = lax.axis_size("lat")
    latitudes = band_rows * bands
    position = lax.axis_index("lat")
    zonal_gain = polar_gain(latitudes, position * band_rows, band_rows)
    diagonal = diag_shift + level_scale[:, None, None] * (2.0 * zonal_gain[None, :, None] + 2.5)
    per_device = WAVES // bands
    columns = jnp.arange(2 * WAVES, dtype=jnp.int32)
    remainder = columns % (2 * per_device)
    wavenumber = columns // (2 * per_device) * per_device + remainder % per_device
    fourier = fourier_table(longitudes, wavenumber, remainder < per_device)
    sines = sine_table(latitudes)
    local_columns = jnp.arange(2 * per_device, dtype=jnp.int32)
    local_waves = position * per_device + local_columns % per_device
    spectral = spectral_weights(latitudes, longitudes, local_waves)

    def apply_operator(field):
        return operate(field, diagonal, level_scale, zonal_gain)

    def apply_inverse(current):
        return precondition(current, diagonal, fourier, sines, spectral)

    solution = jnp.zeros_like(right_side)
    residual = right_side
    adjusted = apply_inverse(residual)
    applied = apply_operator(adjusted)
    aligned, curvature = paired_products(residual, adjusted, applied)
    step_size = aligned / curvature
    direction, image = (adjusted, applied)
    for iteration in range(ITERS):
        solution = solution + step_size * direction
        residual = residual - step_size * image
        if iteration + 1 < ITERS:
            adjusted = apply_inverse(residual)
            applied = apply_operator(adjusted)
            aligned_next, curvature = paired_products(residual, adjusted, applied)
            beta_ratio = aligned_next / aligned
            step_size = aligned_next / (curvature - beta_ratio * aligned_next / step_size)
            direction = adjusted + beta_ratio * direction
            image = applied + beta_ratio * image
            aligned = aligned_next
    return (solution, residual)


def solution(mesh):
    placed = (P("lev", "lat", None), P("lev", "lat", None), P("lev"))
    return jax.shard_map(
        body,
        mesh=mesh,
        in_specs=placed,
        out_specs=(P("lev", "lat", None), P("lev", "lat", None)),
        check_vma=False,
    )
```

profile of v0, /device:TPU:0, one launch (start us, length us, event | category | flops | bytes accessed | tf_op | source)
XLA Modules:
  0.0 550.7 jit_solution(15155512000663679863)
XLA Ops:
  0.7 47.8 %fusion.17 = f32[2,8,1280]{2,1,0:T(8,128)S(1)} fusion(s32[1280]{0:T(1024)S(1)} %fusion.99, pred[1280]{0:T(1024)(128)(4,1)S(1)} %fusion.104, f32[2,8,2048]{2,1,0:T(8,128)} %param.3), kind=kOutput, calls=%fused_computation.21 | convolution fusion | flops 542638080 | bytes 219392 | tf_op jit(solution)/shard_map/dot_general | solution.py:77
  48.5 0.6 copy.36
  49.1 2.8 reshape.181
  51.9 7.6 %all-to-all-start = ((f32[8,1,2560]{2,1,0:T(1,128)}), f32[8,1,2560]{2,1,0:T(1,128)S(1)}, u32[]{:S(2)}, u32[]{:S(2)}) async-start(f32[8,1,2560]{2,1,0:T(1,128)} %reshape.181), calls=%async_computation | async-start | bytes 163840 | tf_op jit(solution)/shard_map/all_to_all | solution.py:88
  59.7 6.7 %all-to-all-done = f32[8,1,2560]{2,1,0:T(1,128)S(1)} async-done(((f32[8,1,2560]{2,1,0:T(1,128)}), f32[8,1,2560]{2,1,0:T(1,128)S(1)}, u32[]{:S(2)}, u32[]{:S(2)}) %all-to-all-start) | async-done | bytes 81952 | tf_op jit(solution)/shard_map/all_to_all | solution.py:88
  66.4 0.5 broadcast.345
  66.9 0.8 reduce
  67.8 2.0 reshape.182
  69.8 0.7 copy.59
  70.5 0.5 fusion.29
  71.0 0.4 convolution_bitcast_fusion.2
  71.5 0.8 copy.40
  72.3 3.4 all-to-all-start.1
  75.8 7.1 %all-to-all-done.1 = f32[2,64,160]{2,0,1:T(2,128)S(1)} async-done(((f32[2,64,160]{2,0,1:T(2,128)}), f32[2,64,160]{2,0,1:T(2,128)S(1)}, u32[]{:S(2)}, u32[]{:S(2)}) %all-to-all-start.1) | async-done | bytes 81952 | tf_op jit(solution)/shard_map/all_to_all | solution.py:85
  83.0 0.1 dot_general.48
  83.1 50.1 %fusion.18 = f32[2,8,2048]{2,1,0:T(8,128)S(1)} fusion(f32[2,8,1280]{2,1,0:T(8,128)S(1)} %dot_general.48, s32[1280]{0:T(1024)S(1)} %fusion.99, pred[1280]{0:T(1024)(128)(4,1)S(1)} %fusion.104, f32[2,8,2048]{2,1,0:T(8,128)S(1)} %copy-done.1, f32[2,8,2048]{2,1,0:T(8,128)S(1)} %copy-done, f32[2,8]{1,0:T(2,128)S(1)} %broadcast_multiply_fusion), kind=kOutput, calls=%fused_computation.22 | convolution fusion | flops 542769152 | bytes 481600 | tf_op jit(solution)/shard_map/dot_general | solution.py:90
  133.3 0.1 fusion.174
  133.4 2.1 collective-permute-start
  135.6 1.3 collective-permute-start.1
  136.9 4.2 collective-permute-done.1
  141.3 0.1 fusion.176
  141.4 0.8 multiply_reduce_fusion.4
  142.2 49.2 %all-reduce.2 = (f32[]{:T(128)}, f32[]{:T(128)}) all-reduce(f32[]{:T(128)} %get-tuple-element.7, f32[]{:T(128)} %get-tuple-element.6), channel_id=1, replica_groups=mesh['lat'=8,'lev'=4] {'lat','lev'}, use_global_device_ids=true, to_apply=%region_1.2 | all-reduce | flops 2 | bytes 16 | tf_op jit(solution)/shard_map/psum | solution.py:101
  192.8 46.1 %fusion.9 = f32[2,8,1280]{2,1,0:T(8,128)S(1)} fusion(f32[2,8,2048]{2,1,0:T(8,128)S(1)} %multiply_subtract_fusion.2, s32[1280]{0:T(1024)S(1)} %fusion.99, pred[1280]{0:T(1024)(128)(4,1)S(1)} %fusion.104), kind=kOutput, calls=%fused_computation.12 | convolution fusion | flops 542638080 | bytes 219392 | tf_op jit(solution)/shard_map/dot_general | solution.py:77
  238.9 0.6 copy.42
  239.6 2.1 reshape.183
  241.7 11.4 %all_to_all.99 = f32[8,1,2560]{2,1,0:T(1,128)S(1)} all-to-all(f32[8,1,2560]{2,1,0:T(1,128)S(1)} %reshape.183), channel_id=1, replica_groups=mesh['lat'=8,'lev'=4] {'lat'}, dimensions={0} | all-to-all | bytes 163840 | tf_op jit(solution)/shard_map/all_to_all | solution.py:88
  253.1 0.8 reduce.1
  254.0 2.0 reshape.184
  256.0 0.7 copy.62
  256.7 0.5 fusion.28
  257.2 0.4 convolution_bitcast_fusion.1
  257.7 0.1 copy.46
  257.8 9.7 %all_to_all.100 = f32[2,64,160]{2,0,1:T(2,128)S(1)} all-to-all(f32[2,64,160]{2,0,1:T(2,128)S(1)} %copy.46), channel_id=1, replica_groups=mesh['lat'=8,'lev'=4] {'lat'}, dimensions={1} | all-to-all | bytes 163840 | tf_op jit(solution)/shard_map/all_to_all | solution.py:85
  267.6 0.1 dot_general.53
  267.7 50.1 %fusion.21 = f32[2,8,2048]{2,1,0:T(8,128)S(1)} fusion(f32[2,8,1280]{2,1,0:T(8,128)S(1)} %dot_general.53, s32[1280]{0:T(1024)S(1)} %fusion.99, pred[1280]{0:T(1024)(128)(4,1)S(1)} %fusion.104, f32[2,8,2048]{2,1,0:T(8,128)S(1)} %multiply_subtract_fusion.2, f32[2,8,2048]{2,1,0:T(8,128)S(1)} %copy-done, f32[2,8]{1,0:T(2,128)S(1)} %broadcast_multiply_fusion), kind=kOutput, calls=%fused_computation.23 | convolution fusion | flops 542769152 | bytes 481600 | tf_op jit(solution)/shard_map/dot_general | solution.py:90
  317.8 0.1 fusion.168
  317.9 2.1 collective-permute-start.2
  320.1 1.3 collective-permute-start.3
  321.5 4.2 collective-permute-done.3
  325.9 0.1 fusion.170
  326.0 0.9 multiply_reduce_fusion.2
  326.9 40.1 %all-reduce.1 = (f32[]{:T(128)}, f32[]{:T(128)}) all-reduce(f32[]{:T(128)} %get-tuple-element.5, f32[]{:T(128)} %get-tuple-element.4), channel_id=1, replica_groups=mesh['lat'=8,'lev'=4] {'lat','lev'}, use_global_device_ids=true, to_apply=%region_5.6 | all-reduce | flops 2 | bytes 16 | tf_op jit(solution)/shard_map/psum | solution.py:101
  371.4 46.1 %fusion.5 = f32[2,8,1280]{2,1,0:T(8,128)S(1)} fusion(f32[2,8,2048]{2,1,0:T(8,128)S(1)} %multiply_subtract_fusion.1, s32[1280]{0:T(1024)S(1)} %fusion.99, pred[1280]{0:T(1024)(128)(4,1)S(1)} %fusion.104), kind=kOutput, calls=%fused_computation.8 | convolution fusion | flops 542638080 | bytes 219392 | tf_op jit(solution)/shard_map/dot_general | solution.py:77
  417.5 0.6 copy.48
  418.2 2.1 reshape.185
  420.3 11.4 %all_to_all.101 = f32[8,1,2560]{2,1,0:T(1,128)S(1)} all-to-all(f32[8,1,2560]{2,1,0:T(1,128)S(1)} %reshape.185), channel_id=1, replica_groups=mesh['lat'=8,'lev'=4] {'lat'}, dimensions={0} | all-to-all | bytes 163840 | tf_op jit(solution)/shard_map/all_to_all | solution.py:88
  431.7 0.8 reduce.2
  432.6 2.0 reshape.186
  434.6 0.7 copy.65
  435.3 0.5 fusion.27
  435.8 0.4 convolution_bitcast_fusion
  436.2 0.1 copy.52
  436.4 9.7 %all_to_all.102 = f32[2,64,160]{2,0,1:T(2,128)S(1)} all-to-all(f32[2,64,160]{2,0,1:T(2,128)S(1)} %copy.52), channel_id=1, replica_groups=mesh['lat'=8,'lev'=4] {'lat'}, dimensions={1} | all-to-all | bytes 163840 | tf_op jit(solution)/shard_map/all_to_all | solution.py:85
  446.2 0.1 dot_general.58
  446.3 50.1 %fusion.24 = f32[2,8,2048]{2,1,0:T(8,128)S(1)} fusion(f32[2,8,1280]{2,1,0:T(8,128)S(1)} %dot_general.58, s32[1280]{0:T(1024)S(1)} %fusion.99, pred[1280]{0:T(1024)(128)(4,1)S(1)} %fusion.104, f32[2,8,2048]{2,1,0:T(8,128)S(1)} %multiply_subtract_fusion.1, f32[2,8,2048]{2,1,0:T(8,128)S(1)} %copy-done, f32[2,8]{1,0:T(2,128)S(1)} %broadcast_multiply_fusion), kind=kOutput, calls=%fused_computation.24 | convolution fusion | flops 542769152 | bytes 481600 | tf_op jit(solution)/shard_map/dot_general | solution.py:90
  496.4 0.1 fusion.162
  496.5 2.1 collective-permute-start.4
  498.7 1.3 collective-permute-start.5
  500.1 4.2 collective-permute-done.5
  504.5 0.1 fusion.164
  504.6 0.8 multiply_reduce_fusion
  505.4 40.3 %all-reduce = (f32[]{:T(128)}, f32[]{:T(128)}) all-reduce(f32[]{:T(128)} %get-tuple-element.3, f32[]{:T(128)} %get-tuple-element.2), channel_id=1, replica_groups=mesh['lat'=8,'lev'=4] {'lat','lev'}, use_global_device_ids=true, to_apply=%region_9.10 | all-reduce | flops 2 | bytes 16 | tf_op jit(solution)/shard_map/psum | solution.py:101
  549.6 0.8 multiply_subtract_fusion
  (44 shorter events, 1.8 us)
Async XLA Ops:
  51.9 14.5 %all-to-all-start = ((f32[8,1,2560]{2,1,0:T(1,128)}), f32[8,1,2560]{2,1,0:T(1,128)S(1)}, u32[]{:S(2)}, u32[]{:S(2)}) async-start(f32[8,1,2560]{2,1,0:T(1,128)} %reshape.181), calls=%async_computation | async-start | bytes 163840 | tf_op jit(solution)/shard_map/all_to_all | solution.py:88
  69.8 5.9 %copy-start.2 = (f32[2]{0:T(128)S(1)}, f32[2]{0:T(128)}, u32[]{:S(2)}) copy-start(f32[2]{0:T(128)} %param.5) | copy-start | bytes 28
  69.8 13.3 %copy-start = (f32[2,8,2048]{2,1,0:T(8,128)S(1)}, f32[2,8,2048]{2,1,0:T(8,128)}, u32[]{:S(2)}) copy-start(f32[2,8,2048]{2,1,0:T(8,128)} %param.4) | copy-start | bytes 393220
  69.8 13.3 %copy-start.1 = (f32[2,8,2048]{2,1,0:T(8,128)S(1)}, f32[2,8,2048]{2,1,0:T(8,128)}, u32[]{:S(2)}) copy-start(f32[2,8,2048]{2,1,0:T(8,128)} %param.3) | copy-start | bytes 393220
  72.3 10.7 %all-to-all-start.1 = ((f32[2,64,160]{2,0,1:T(2,128)}), f32[2,64,160]{2,0,1:T(2,128)S(1)}, u32[]{:S(2)}, u32[]{:S(2)}) async-start(f32[2,64,160]{2,0,1:T(2,128)} %copy.40), calls=%async_computation.1 | async-start | bytes 262144 | tf_op jit(solution)/shard_map/all_to_all | solution.py:85
  133.4 3.6 collective-permute-start
  135.6 5.6 %collective-permute-start.1 = (f32[2,1,2048]{2,1,0:T(1,128)S(1)}, f32[2,1,2048]{2,1,0:T(1,128)S(1)}, u32[]{:S(2)}, u32[]{:S(2)}) collective-permute-start(f32[2,1,2048]{2,1,0:T(1,128)S(1)} %get-tuple-element.58), channel_id=1, source_target_pairs={{4,0},{8,4},{12,8},{16,12},{20,16},{24,20},{28,24},{5,1},{9,5},{13... | collective-permute-start | bytes 49160 | tf_op jit(solution)/shard_map/ppermute | solution.py:18
  317.9 3.6 collective-permute-start.2
  320.1 5.6 %collective-permute-start.3 = (f32[2,1,2048]{2,1,0:T(1,128)S(1)}, f32[2,1,2048]{2,1,0:T(1,128)S(1)}, u32[]{:S(2)}, u32[]{:S(2)}) collective-permute-start(f32[2,1,2048]{2,1,0:T(1,128)S(1)} %get-tuple-element.44), channel_id=1, source_target_pairs={{4,0},{8,4},{12,8},{16,12},{20,16},{24,20},{28,24},{5,1},{9,5},{13... | collective-permute-start | bytes 49160 | tf_op jit(solution)/shard_map/ppermute | solution.py:18
  496.5 3.6 collective-permute-start.4
  498.7 5.6 %collective-permute-start.5 = (f32[2,1,2048]{2,1,0:T(1,128)S(1)}, f32[2,1,2048]{2,1,0:T(1,128)S(1)}, u32[]{:S(2)}, u32[]{:S(2)}) collective-permute-start(f32[2,1,2048]{2,1,0:T(1,128)S(1)} %get-tuple-element.30), channel_id=1, source_target_pairs={{4,0},{8,4},{12,8},{16,12},{20,16},{24,20},{28,24},{5,1},{9,5},{13... | collective-permute-start | bytes 49160 | tf_op jit(solution)/shard_map/ppermute | solution.py:18
where the time goes:
time: 560 us; the launch traced here: 551 us
  matrix products  293 us (52%)
  blocking collectives  172 us (31%)
  waiting for transfers between devices  26.8 us (5%)
  starting transfers between devices  21.1 us (4%)
  local copies, waits for them, and re-layouts  20.1 us (4%)
  between operations  11.2 us (2%)
  other arithmetic  6.44 us (1%)
    dot_general x3, matrix products, precondition(): lax.dot_general(arrived.reshape(levels * band_rows, columns), fourier, ((...  150 us
    dot_general x3, matrix products, precondition(): jnp.dot(flattened, fourier, precision=highest, preferred_element_type=jnp...  140 us
    psum x3, blocking collectives, paired_products(): lax.psum((jnp.sum(residual * adjusted), jnp.sum(applied * adjusted)), ('l...  130 us
    all_to_all x2, blocking collectives, precondition(): lax.all_to_all(coefficients, 'lat', split_axis=2, concat_axis=1, tiled=True)  22.9 us
    all_to_all x2, blocking collectives, meridional(): lax.all_to_all(returned, 'lat', split_axis=1, concat_axis=2, tiled=True)  19.5 us
    unnamed x12, local copies, waits for them, and re-layouts  13 us
    ppermute x3, waiting for transfers between devices, with_halo(): lax.ppermute(lax.slice_in_dim(block, 0, width, axis=dim), axis, backward)  12.7 us
  transfers between devices with their start and end apart: 8, of which 8 were waited for; matrix products, arithmetic and copies ran while one was open for 0% of the time, Pallas kernels for 0%

commit v1 on v0

--- a/solution.py
+++ b/solution.py
@@ -85,7 +85,12 @@
         return lax.all_to_all(returned, "lat", split_axis=1, concat_axis=2, tiled=True)
 
     arrived = meridional(
-        lax.all_to_all(coefficients, "lat", split_axis=2, concat_axis=1, tiled=True)
+        jnp.concatenate(
+            lax.all_to_all(
+                jnp.stack(jnp.split(coefficients, lax.axis_size("lat"), axis=2)), "lat", 0, 0
+            ),
+            axis=1,
+        )
     )
     synthesis = lax.dot_general(
         arrived.reshape(levels * band_rows, columns),

time: 560 us -> 540 us (0.964)
  local copies, waits for them, and re-layouts: 20.1 us -> 9.62 us
  blocking collectives: 172 us -> 165 us
    psum x3, blocking collectives: 130 us -> 121 us  [paired_products(): lax.psum((jnp.sum(residual * adjusted), jnp.sum(applied * adjusted)), ('l...]
    unnamed x12 -> x27, local copies, waits for them, and re-layouts: 13 us -> 6.16 us
where the time goes in v1:
time: 540 us; the launch traced here: 531 us
  matrix products  293 us (54%)
  blocking collectives  165 us (31%)
  waiting for transfers between devices  27.1 us (5%)
  starting transfers between devices  21.2 us (4%)
  between operations  10.9 us (2%)
  local copies, waits for them, and re-layouts  9.62 us (2%)
    dot_general x3, matrix products, precondition(): lax.dot_general(arrived.reshape(levels * band_rows, columns), fourier, ((...  150 us
    dot_general x3, matrix products, precondition(): jnp.dot(flattened, fourier, precision=highest, preferred_element_type=jnp...  140 us
    psum x3, blocking collectives, paired_products(): lax.psum((jnp.sum(residual * adjusted), jnp.sum(applied * adjusted)), ('l...  121 us
    all_to_all x2, blocking collectives, precondition(): lax.all_to_all(jnp.stack(jnp.split(coefficients, lax.axis_size('lat'), ax...  23.5 us
    all_to_all x2, blocking collectives, meridional(): lax.all_to_all(returned, 'lat', split_axis=1, concat_axis=2, tiled=True)  19.9 us
    ppermute x3, waiting for transfers between devices, with_halo(): lax.ppermute(lax.slice_in_dim(block, 0, width, axis=dim), axis, backward)  12.7 us
  transfers between devices with their start and end apart: 8, of which 8 were waited for; matrix products, arithmetic and copies ran while one was open for 0% of the time, Pallas kernels for 0%

profile of v1, /device:TPU:0, one launch (start us, length us, event | category | flops | bytes accessed | tf_op | source)
XLA Modules:
  0.0 530.7 jit_solution(12528083210708488351)
XLA Ops:
  0.7 47.8 %fusion.17 = f32[2,8,1280]{2,1,0:T(8,128)S(1)} fusion(s32[1280]{0:T(1024)S(1)} %fusion.102, pred[1280]{0:T(1024)(128)(4,1)S(1)} %fusion.107, f32[2,8,2048]{2,1,0:T(8,128)} %param.3), kind=kOutput, calls=%fused_computation.21 | convolution fusion | flops 542638080 | bytes 219392 | tf_op jit(solution)/shard_map/dot_general | solution.py:77
  48.5 0.6 constant_dynamic-update-slice_fusion.7
  49.1 0.7 constant_dynamic-update-slice_fusion.6
  49.8 0.7 constant_dynamic-update-slice_fusion.5
  50.5 0.7 constant_dynamic-update-slice_fusion.4
  51.1 0.6 constant_dynamic-update-slice_fusion.3
  51.7 0.7 constant_dynamic-update-slice_fusion.2
  52.4 0.7 constant_dynamic-update-slice_fusion.1
  53.1 0.7 constant_dynamic-update-slice_fusion
  53.8 7.3 %all-to-all-start = ((f32[8,2,8,160]{3,2,1,0:T(8,128)}), f32[8,2,8,160]{3,2,1,0:T(8,128)S(1)}, u32[]{:S(2)}, u32[]{:S(2)}) async-start(f32[8,2,8,160]{3,2,1,0:T(8,128)} %constant_dynamic-update-slice_fusion), calls=%async_computation | async-start | bytes 262144 | tf_op jit(solution)/shard_map/all_to_all | solution.py:89
  61.2 0.1 add_divide_fusion
  61.3 7.1 %all-to-all-done = f32[8,2,8,160]{3,2,1,0:T(8,128)S(1)} async-done(((f32[8,2,8,160]{3,2,1,0:T(8,128)}), f32[8,2,8,160]{3,2,1,0:T(8,128)S(1)}, u32[]{:S(2)}, u32[]{:S(2)}) %all-to-all-start) | async-done | bytes 81952 | tf_op jit(solution)/shard_map/all_to_all | solution.py:89
  68.4 0.5 fusion.29
  68.9 0.4 convolution_bitcast_fusion.2
  69.4 0.8 copy.22
  70.1 3.7 all-to-all-start.1
  74.0 7.1 %all-to-all-done.1 = f32[2,64,160]{2,0,1:T(2,128)S(1)} async-done(((f32[2,64,160]{2,0,1:T(2,128)}), f32[2,64,160]{2,0,1:T(2,128)S(1)}, u32[]{:S(2)}, u32[]{:S(2)}) %all-to-all-start.1) | async-done | bytes 81952 | tf_op jit(solution)/shard_map/all_to_all | solution.py:85
  81.1 0.1 copy.55
  81.2 0.1 dot_general.48
  81.3 0.7 copy-done.1
  82.0 0.1 copy-done
  82.1 50.0 %fusion.18 = f32[2,8,2048]{2,1,0:T(8,128)S(1)} fusion(f32[2,8,1280]{2,1,0:T(8,128)S(1)} %dot_general.48, s32[1280]{0:T(1024)S(1)} %fusion.102, pred[1280]{0:T(1024)(128)(4,1)S(1)} %fusion.107, f32[2,8,2048]{2,1,0:T(8,128)S(1)} %copy-done.1, f32[2,8,2048]{2,1,0:T(8,128)S(1)} %copy-done, f32[2,8]{1,0:T(2,128)S(1)} %broadcast_multiply_fusion), kind=kOutput, calls=%fused_computation.22 | convolution fusion | flops 542769152 | bytes 481600 | tf_op jit(solution)/shard_map/dot_general | solution.py:95
  132.3 0.1 fusion.177
  132.4 2.1 collective-permute-start
  134.5 0.1 fusion.176
  134.6 1.3 collective-permute-start.1
  135.9 4.2 collective-permute-done.1
  140.3 0.1 fusion.178
  140.3 0.1 fusion.179
  140.4 0.8 multiply_reduce_fusion.4
  141.2 40.9 %all-reduce.2 = (f32[]{:T(128)}, f32[]{:T(128)}) all-reduce(f32[]{:T(128)} %get-tuple-element.7, f32[]{:T(128)} %get-tuple-element.6), channel_id=1, replica_groups=mesh['lat'=8,'lev'=4] {'lat','lev'}, use_global_device_ids=true, to_apply=%region_1.2 | all-reduce | flops 2 | bytes 16 | tf_op jit(solution)/shard_map/psum | solution.py:106
  183.5 46.1 %fusion.9 = f32[2,8,1280]{2,1,0:T(8,128)S(1)} fusion(f32[2,8,2048]{2,1,0:T(8,128)S(1)} %multiply_subtract_fusion.2, s32[1280]{0:T(1024)S(1)} %fusion.102, pred[1280]{0:T(1024)(128)(4,1)S(1)} %fusion.107), kind=kOutput, calls=%fused_computation.12 | convolution fusion | flops 542638080 | bytes 219392 | tf_op jit(solution)/shard_map/dot_general | solution.py:77
  230.1 11.8 %all_to_all.60 = f32[8,2,8,160]{3,2,1,0:T(8,128)S(1)} all-to-all(f32[8,2,8,160]{3,2,1,0:T(8,128)S(1)} %constant_dynamic-update-slice_fusion.8), channel_id=1, replica_groups=mesh['lat'=8,'lev'=4] {'lat'}, dimensions={0} | all-to-all | bytes 163840 | tf_op jit(solution)/shard_map/all_to_all | solution.py:89
  241.8 0.5 fusion.28
  242.3 0.5 convolution_bitcast_fusion.1
  242.8 0.1 copy.26
  242.9 9.9 %all_to_all.61 = f32[2,64,160]{2,0,1:T(2,128)S(1)} all-to-all(f32[2,64,160]{2,0,1:T(2,128)S(1)} %copy.26), channel_id=1, replica_groups=mesh['lat'=8,'lev'=4] {'lat'}, dimensions={1} | all-to-all | bytes 163840 | tf_op jit(solution)/shard_map/all_to_all | solution.py:85
  252.8 0.1 copy.54
  252.9 0.1 dot_general.53
  253.0 50.1 %fusion.21 = f32[2,8,2048]{2,1,0:T(8,128)S(1)} fusion(f32[2,8,1280]{2,1,0:T(8,128)S(1)} %dot_general.53, s32[1280]{0:T(1024)S(1)} %fusion.102, pred[1280]{0:T(1024)(128)(4,1)S(1)} %fusion.107, f32[2,8,2048]{2,1,0:T(8,128)S(1)} %multiply_subtract_fusion.2, f32[2,8,2048]{2,1,0:T(8,128)S(1)} %copy-done, f32[2,8]{1,0:T(2,128)S(1)} %broadcast_multiply_fusion), kind=kOutput, calls=%fused_computation.23 | convolution fusion | flops 542769152 | bytes 481600 | tf_op jit(solution)/shard_map/dot_general | solution.py:95
  303.1 0.1 fusion.171
  303.2 2.1 collective-permute-start.2
  305.4 1.3 collective-permute-start.3
  306.8 4.2 collective-permute-done.3
  311.2 0.1 fusion.173
  311.3 0.8 multiply_reduce_fusion.2
  312.2 39.9 %all-reduce.1 = (f32[]{:T(128)}, f32[]{:T(128)}) all-reduce(f32[]{:T(128)} %get-tuple-element.5, f32[]{:T(128)} %get-tuple-element.4), channel_id=1, replica_groups=mesh['lat'=8,'lev'=4] {'lat','lev'}, use_global_device_ids=true, to_apply=%region_5.6 | all-reduce | flops 2 | bytes 16 | tf_op jit(solution)/shard_map/psum | solution.py:106
  356.5 46.1 %fusion.5 = f32[2,8,1280]{2,1,0:T(8,128)S(1)} fusion(f32[2,8,2048]{2,1,0:T(8,128)S(1)} %multiply_subtract_fusion.1, s32[1280]{0:T(1024)S(1)} %fusion.102, pred[1280]{0:T(1024)(128)(4,1)S(1)} %fusion.107), kind=kOutput, calls=%fused_computation.8 | convolution fusion | flops 542638080 | bytes 219392 | tf_op jit(solution)/shard_map/dot_general | solution.py:77
  403.0 11.8 %all_to_all.62 = f32[8,2,8,160]{3,2,1,0:T(8,128)S(1)} all-to-all(f32[8,2,8,160]{3,2,1,0:T(8,128)S(1)} %constant_dynamic-update-slice_fusion.16), channel_id=1, replica_groups=mesh['lat'=8,'lev'=4] {'lat'}, dimensions={0} | all-to-all | bytes 163840 | tf_op jit(solution)/shard_map/all_to_all | solution.py:89
  414.8 0.5 fusion.27
  415.4 0.5 convolution_bitcast_fusion
  415.8 0.1 copy.30
  415.9 10.0 %all_to_all.63 = f32[2,64,160]{2,0,1:T(2,128)S(1)} all-to-all(f32[2,64,160]{2,0,1:T(2,128)S(1)} %copy.30), channel_id=1, replica_groups=mesh['lat'=8,'lev'=4] {'lat'}, dimensions={1} | all-to-all | bytes 163840 | tf_op jit(solution)/shard_map/all_to_all | solution.py:85
  425.9 0.1 copy.53
  426.0 0.1 dot_general.58
  426.1 50.1 %fusion.24 = f32[2,8,2048]{2,1,0:T(8,128)S(1)} fusion(f32[2,8,1280]{2,1,0:T(8,128)S(1)} %dot_general.58, s32[1280]{0:T(1024)S(1)} %fusion.102, pred[1280]{0:T(1024)(128)(4,1)S(1)} %fusion.107, f32[2,8,2048]{2,1,0:T(8,128)S(1)} %multiply_subtract_fusion.1, f32[2,8,2048]{2,1,0:T(8,128)S(1)} %copy-done, f32[2,8]{1,0:T(2,128)S(1)} %broadcast_multiply_fusion), kind=kOutput, calls=%fused_computation.24 | convolution fusion | flops 542769152 | bytes 481600 | tf_op jit(solution)/shard_map/dot_general | solution.py:95
  476.2 0.1 fusion.165
  476.3 2.1 collective-permute-start.4
  478.5 1.3 collective-permute-start.5
  479.9 4.2 collective-permute-done.5
  484.3 0.1 fusion.167
  484.4 0.8 multiply_reduce_fusion
  485.2 40.5 %all-reduce = (f32[]{:T(128)}, f32[]{:T(128)}) all-reduce(f32[]{:T(128)} %get-tuple-element.3, f32[]{:T(128)} %get-tuple-element.2), channel_id=1, replica_groups=mesh['lat'=8,'lev'=4] {'lat','lev'}, use_global_device_ids=true, to_apply=%region_9.10 | all-reduce | flops 2 | bytes 16 | tf_op jit(solution)/shard_map/psum | solution.py:106
  529.5 0.8 multiply_subtract_fusion
  (52 shorter events, 2.2 us)
Async XLA Ops:
  53.8 14.6 %all-to-all-start = ((f32[8,2,8,160]{3,2,1,0:T(8,128)}), f32[8,2,8,160]{3,2,1,0:T(8,128)S(1)}, u32[]{:S(2)}, u32[]{:S(2)}) async-start(f32[8,2,8,160]{3,2,1,0:T(8,128)} %constant_dynamic-update-slice_fusion), calls=%async_computation | async-start | bytes 262144 | tf_op jit(solution)/shard_map/all_to_all | solution.py:89
  70.1 3.7 copy-start.2
  70.1 11.0 %all-to-all-start.1 = ((f32[2,64,160]{2,0,1:T(2,128)}), f32[2,64,160]{2,0,1:T(2,128)S(1)}, u32[]{:S(2)}, u32[]{:S(2)}) async-start(f32[2,64,160]{2,0,1:T(2,128)} %copy.22), calls=%async_computation.1 | async-start | bytes 262144 | tf_op jit(solution)/shard_map/all_to_all | solution.py:85
  81.1 0.9 copy-start.1
  81.2 0.9 copy-start
  132.4 3.6 collective-permute-start
  134.6 5.6 %collective-permute-start.1 = (f32[2,1,2048]{2,1,0:T(1,128)S(1)}, f32[2,1,2048]{2,1,0:T(1,128)S(1)}, u32[]{:S(2)}, u32[]{:S(2)}) collective-permute-start(f32[2,1,2048]{2,1,0:T(1,128)S(1)} %get-tuple-element.58), channel_id=1, source_target_pairs={{4,0},{8,4},{12,8},{16,12},{20,16},{24,20},{28,24},{5,1},{9,5},{13... | collective-permute-start | bytes 49160 | tf_op jit(solution)/shard_map/ppermute | solution.py:18
  303.2 3.6 collective-permute-start.2
  305.4 5.6 %collective-permute-start.3 = (f32[2,1,2048]{2,1,0:T(1,128)S(1)}, f32[2,1,2048]{2,1,0:T(1,128)S(1)}, u32[]{:S(2)}, u32[]{:S(2)}) collective-permute-start(f32[2,1,2048]{2,1,0:T(1,128)S(1)} %get-tuple-element.44), channel_id=1, source_target_pairs={{4,0},{8,4},{12,8},{16,12},{20,16},{24,20},{28,24},{5,1},{9,5},{13... | collective-permute-start | bytes 49160 | tf_op jit(solution)/shard_map/ppermute | solution.py:18
  476.3 3.6 collective-permute-start.4
  478.5 5.6 %collective-permute-start.5 = (f32[2,1,2048]{2,1,0:T(1,128)S(1)}, f32[2,1,2048]{2,1,0:T(1,128)S(1)}, u32[]{:S(2)}, u32[]{:S(2)}) collective-permute-start(f32[2,1,2048]{2,1,0:T(1,128)S(1)} %get-tuple-element.30), channel_id=1, source_target_pairs={{4,0},{8,4},{12,8},{16,12},{20,16},{24,20},{28,24},{5,1},{9,5},{13... | collective-permute-start | bytes 49160 | tf_op jit(solution)/shard_map/ppermute | solution.py:18
